TPU v7x, 32 devices: a whole 2x2x4 slice. The times are simulated.
32 devices in a mesh: gx: 2 (over y), gy: 4 (over z), gz: 4 (over x, core).
Axes of the slice: x: 2, y: 2, z: 4, core: 2. Of those that a mesh axis runs over, the one named last changes fastest.
Arguments:
- kappa_sq: float32 [32, 64, 512], P('gx', 'gz', 'gy'), may hold values from 0.004 to 0.4
- probe_bits: int32 [4, 32, 64, 512], P(None, 'gx', 'gz', 'gy'), may hold values from 0 to 1
Outputs:
- solution: float32 [4, 32, 64, 512], P(None, 'gx', 'gz', 'gy')
- relative_residual: float32 [4], replicated
All inputs are finite; a program needn't handle non-finite values.
Results may differ from a plain program's by a relative error of at most 0.0001.
Values sent between devices are 32-bit elements; how exact they have to be, the bound alone decides.
A program may use at most 128 MiB of HBM per device.

v0:
```python
import jax
import jax.numpy as jnp
from jax import lax
from jax.sharding import PartitionSpec as P

LEVELS = 3
COARSE_SWEEPS = 8
ITERS = 2
damping = 0.8


def extended(block, sides, width):
    for axis, dim in sides:
        count = lax.axis_size(axis)
        forward = [(i, i + 1) for i in range(count - 1)]
        backward = [(target, source) for source, target in forward]
        low = lax.ppermute(
            lax.slice_in_dim(block, block.shape[dim] - width, None, axis=dim), axis, forward
        )
        high = lax.ppermute(lax.slice_in_dim(block, 0, width, axis=dim), axis, backward)
        block = jnp.concatenate([low, block, high], axis=dim)
    return block


def neighbours(padded):
    along_first = padded[..., 2:, 1:-1, 1:-1] + padded[..., :-2, 1:-1, 1:-1]
    along_second = padded[..., 1:-1, 2:, 1:-1] + padded[..., 1:-1, :-2, 1:-1]
    along_third = padded[..., 1:-1, 1:-1, 2:] + padded[..., 1:-1, 1:-1, :-2]
    return along_first + along_second + along_third


def coarsen(field):
    leading = field.shape[:-3]
    cells_first, cells_second, cells_third = field.shape[-3:]
    grouped = field.reshape(
        leading + (cells_first // 2, 2, cells_second // 2, 2, cells_third // 2, 2)
    )
    return jnp.mean(grouped, axis=(-5, -3, -1))


def refine(field):
    leading = field.shape[:-3]
    cells_first, cells_second, cells_third = field.shape[-3:]
    spread = field.reshape(leading + (cells_first, 1, cells_second, 1, cells_third, 1))
    spread = jnp.broadcast_to(spread, leading + (cells_first, 2, cells_second, 2, cells_third, 2))
    return spread.reshape(leading + (cells_first * 2, cells_second * 2, cells_third * 2))


def level_faces(field, grid_level):
    if grid_level == 0:
        return extended(field, (("gx", 1), ("gy", 3), ("gz", 2)), 1)
    return extended(field, (("gx", 1), ("gy", 3), ("gz", 2)), 1)


def operate(field, diagonal, coupling, grid_level):
    return diagonal * field - coupling * neighbours(level_faces(field, grid_level))


def jacobi_sweep(field, rhs_field, diagonal, coupling, grid_level):
    return field + damping * (rhs_field - operate(field, diagonal, coupling, grid_level)) / diagonal


def assemble(gathered):
    count_x = lax.axis_size("gx")
    count_y = lax.axis_size("gy")
    count_z = lax.axis_size("gz")
    leading = gathered.shape[1:-3]
    cells_first, cells_second, cells_third = gathered.shape[-3:]
    lead_count = len(leading)
    blocks = gathered.reshape(
        (count_x, count_y, count_z) + leading + (cells_first, cells_second, cells_third)
    )
    permutation = tuple(range(3, 3 + lead_count)) + (
        0,
        3 + lead_count,
        2,
        4 + lead_count,
        1,
        5 + lead_count,
    )
    blocks = jnp.transpose(blocks, permutation)
    return blocks.reshape(
        leading + (count_x * cells_first, count_z * cells_second, count_y * cells_third)
    )


def local_dot(first_field, second_field):
    return jnp.sum(first_field * second_field, axis=(1, 2, 3))


def expand(values):
    return values[:, None, None, None]


def per_device(kappa_sq, probe_bits):
    diagonals = []
    couplings = []
    coef_field = kappa_sq
    for grid_level in range(LEVELS + 1):
        if grid_level > 0:
            coef_field = coarsen(coef_field)
        coupling = 0.25**grid_level
        diagonals.append(coef_field + 6.0 * coupling)
        couplings.append(coupling)
    global_diag = assemble(
        lax.all_gather(diagonals[LEVELS][None], ("gx", "gy", "gz"), axis=0, tiled=True)
    )

    def coarsest(rhs_field):
        diagonal = diagonals[LEVELS]
        coupling = couplings[LEVELS]
        global_rhs = assemble(
            lax.all_gather(rhs_field[None], ("gx", "gy", "gz"), axis=0, tiled=True)
        )
        field = damping * global_rhs / global_diag
        for sweep_index in range(COARSE_SWEEPS - 1):
            padded = jnp.pad(field, ((0, 0), (1, 1), (1, 1), (1, 1)))
            field = (
                field
                + damping
                * (global_rhs - (global_diag * field - coupling * neighbours(padded)))
                / global_diag
            )
        probes, block_x, block_z, block_y = rhs_field.shape
        zero_index = jnp.zeros((), jnp.int32)
        starts = (
            zero_index,
            lax.axis_index("gx") * block_x,
            lax.axis_index("gz") * block_z,
            lax.axis_index("gy") * block_y,
        )
        return lax.dynamic_slice(field, starts, (probes, block_x, block_z, block_y))

    def vcycle(rhs_field, grid_level):
        if grid_level == LEVELS:
            return coarsest(rhs_field)
        diagonal = diagonals[grid_level]
        coupling = couplings[grid_level]
        field = damping * rhs_field / diagonal
        field = jacobi_sweep(field, rhs_field, diagonal, coupling, grid_level)
        remainder = rhs_field - operate(field, diagonal, coupling, grid_level)
        field = field + refine(vcycle(coarsen(remainder), grid_level + 1))
        field = jacobi_sweep(field, rhs_field, diagonal, coupling, grid_level)
        return jacobi_sweep(field, rhs_field, diagonal, coupling, grid_level)

    right_side = 2.0 * probe_bits.astype(jnp.float32) - 1.0
    solution = jnp.zeros_like(right_side)
    residual = right_side
    fine_diag = diagonals[0]

    def precond_sum(first_field, second_field):
        return lax.psum(local_dot(first_field, second_field), ("gx", "gy", "gz"))

    precond = vcycle(residual, 0)
    precond_dot = precond_sum(residual, precond)
    search = precond
    for iteration in range(ITERS):
        operated = operate(search, fine_diag, 1.0, 0)
        step_size = precond_dot / lax.psum(local_dot(search, operated), ("gx", "gy", "gz"))
        solution = solution + expand(step_size) * search
        residual = residual - expand(step_size) * operated
        if iteration + 1 < ITERS:
            precond = vcycle(residual, 0)
            next_dot = precond_sum(residual, precond)
            search = precond + expand(next_dot / precond_dot) * search
            precond_dot = next_dot
    squares = lax.psum(local_dot(residual, residual), ("gx", "gy", "gz"))
    cell_total = (
        probe_bits.shape[1]
        * probe_bits.shape[2]
        * probe_bits.shape[3]
        * lax.axis_size("gx")
        * lax.axis_size("gy")
        * lax.axis_size("gz")
    )
    return (solution, jnp.sqrt(squares / cell_total))


def solution(mesh):
    return jax.shard_map(
        per_device,
        mesh=mesh,
        in_specs=(P("gx", "gz", "gy"), P(None, "gx", "gz", "gy")),
        out_specs=(P(None, "gx", "gz", "gy"), P()),
        check_vma=False,
    )
```

profile of v0, /device:TPU:0, one launch (start us, length us, event | category | flops | bytes accessed | tf_op | source)
XLA Modules:
  0.0 1080.8 jit_solution(16804115378510842129)
XLA Ops:
  2.7 4.9 collective-permute-start.1
  16.0 4.5 collective-permute-start.2
  40.4 4.8 collective-permute-start.8
  45.2 9.7 reshape.124
  69.1 8.8 copy.1882
  77.9 11.7 %reduce_sum.126 = f32[4,8,8,64]{0,3,2,1:T(8,128)S(1)} reduce(f32[4,8,2,8,2,64,2]{0,6,5,4,3,2,1:T(2,128)} %bitcast.21, f32[]{:T(128)} %constant.28.clone.1), dimensions={2,4,6}, to_apply=%region_0.0 | reduce | flops 114688 | bytes 589828 | tf_op jit(solution)/shard_map/reduce_sum | solution.py:38
  99.1 4.6 collective-permute-start.14
  117.1 4.3 collective-permute-done.18
  122.8 4.7 collective-permute-start.20
  147.8 4.4 collective-permute-start.26
  154.1 4.4 collective-permute-done.27
  168.1 47.4 %all-gather.1 = f32[64,2,16]{2,1,0:T(2,128)S(1)} all-gather(f32[2,2,16]{2,1,0:T(2,128)S(1)} %multiply_add_fusion.3), channel_id=3, replica_groups=mesh['gx'=2,'gy'=4,'gz'=4] {'gx','gy','gz'}, dimensions={0}, use_global_device_ids=true | all-gather | bytes 8448 | tf_op jit(solution)/shard_map/all_gather | solution.py:106
  230.6 40.5 %all-gather = f32[128,2,2,16]{3,2,1,0:T(2,128)S(1)} all-gather(f32[4,2,2,16]{3,2,1,0:T(2,128)S(1)} %copy.1905), channel_id=2, replica_groups=mesh['gx'=2,'gy'=4,'gz'=4] {'gx','gy','gz'}, dimensions={0}, use_global_device_ids=true | all-gather | bytes 33792 | tf_op jit(solution)/shard_map/all_gather | solution.py:113
  283.4 4.3 collective-permute-done.39
  298.5 4.3 collective-permute-done.42
  306.0 4.3 collective-permute-done.45
  328.2 4.6 collective-permute-start.50
  337.1 4.6 collective-permute-start.53
  351.9 4.7 collective-permute-start.56
  361.0 5.0 collective-permute-start.59
  369.5 7.8 broadcast_in_dim.14
  377.3 10.0 copy.1931
  397.7 4.7 collective-permute-start.62
  405.1 4.3 collective-permute-start.65
  410.8 5.8 collective-permute-done.64
  427.6 4.8 collective-permute-start.68
  453.6 4.8 collective-permute-start.74
  469.7 41.7 %all-reduce.14 = (f32[4]{0:T(128)S(1)}, f32[4]{0:T(128)S(1)}) all-reduce(f32[4]{0:T(128)S(1)} %get-tuple-element.13, f32[4]{0:T(128)S(1)} %get-tuple-element.12), channel_id=1, replica_groups=mesh['gx'=2,'gy'=4,'gz'=4] {'gx','gy','gz'}, use_global_device_ids=true, to_apply=%region_7.8 | all-reduce | flops 8 | bytes 64 | tf_op jit(solution)/shard_map/psum | solution.py:152
  524.4 4.5 collective-permute-start.80
  550.0 4.8 collective-permute-start.86
  566.8 8.8 copy.1982
  575.7 13.1 %reduce_sum.134 = f32[4,8,8,64]{0,3,2,1:T(8,128)} reduce(f32[4,8,2,8,2,64,2]{0,6,5,4,3,2,1:T(2,128)} %bitcast.23, f32[]{:T(128)} %constant.28.clone.1), dimensions={2,4,6}, to_apply=%region_10.11 | reduce | flops 114688 | bytes 589828 | tf_op jit(solution)/shard_map/reduce_sum | solution.py:38
  599.8 4.9 collective-permute-start.92
  623.4 4.7 collective-permute-start.98
  652.0 4.4 collective-permute-start.104
  658.3 4.4 collective-permute-done.105
  701.8 44.2 %all-gather.2 = f32[128,2,2,16]{3,2,1,0:T(2,128)S(1)} all-gather(f32[4,2,2,16]{3,2,1,0:T(2,128)S(1)} %copy.2005), channel_id=4, replica_groups=mesh['gx'=2,'gy'=4,'gz'=4] {'gx','gy','gz'}, dimensions={0}, use_global_device_ids=true | all-gather | bytes 33792 | tf_op jit(solution)/shard_map/all_gather | solution.py:113
  815.0 4.6 collective-permute-start.128
  836.9 5.0 collective-permute-start.134
  853.7 8.9 broadcast_in_dim.17
  862.6 10.0 copy.2029
  883.0 5.0 collective-permute-start.140
  893.9 5.8 collective-permute-done.142
  910.7 5.1 collective-permute-start.146
  926.9 41.6 %psum.37 = f32[4]{0:T(128)S(1)} all-reduce(f32[4]{0:T(128)S(1)} %get-tuple-element.18), channel_id=1, replica_groups=mesh['gx'=2,'gy'=4,'gz'=4] {'gx','gy','gz'}, use_global_device_ids=true, to_apply=%region_14.15 | all-reduce | flops 4 | bytes 32 | tf_op jit(solution)/shard_map/psum | solution.py:152
  981.2 4.5 collective-permute-start.152
  996.1 41.6 %psum.38 = f32[4]{0:T(128)S(1)} all-reduce(f32[4]{0:T(128)S(1)} %get-tuple-element.16), channel_id=1, replica_groups=mesh['gx'=2,'gy'=4,'gz'=4] {'gx','gy','gz'}, use_global_device_ids=true, to_apply=%region_16.17 | all-reduce | flops 4 | bytes 32 | tf_op jit(solution)/shard_map/psum | solution.py:159
  1038.8 41.2 %psum.39 = f32[4]{0:T(128)S(1)} all-reduce(f32[4]{0:T(128)S(1)} %get-tuple-element.199), channel_id=1, replica_groups=mesh['gx'=2,'gy'=4,'gz'=4] {'gx','gy','gz'}, use_global_device_ids=true, to_apply=%region_18.19 | all-reduce | flops 4 | bytes 32 | tf_op jit(solution)/shard_map/psum | solution.py:167
  (671 shorter events, 539.1 us)
Async XLA Ops:
  2.7 6.5 collective-permute-start.1
  14.2 6.3 collective-permute-start.3
  38.6 20.4 %collective-permute-start.9 = (f32[4,18,16,1]{1,2,3,0:T(8,128)S(1)}, f32[4,18,16,1]{1,2,3,0:T(8,128)S(1)}, u32[]{:S(2)}, u32[]{:S(2)}) collective-permute-start(f32[4,18,16,1]{1,2,3,0:T(8,128)S(1)} %copy.1873), channel_id=1, source_target_pairs={{4,0},{8,4},{12,8},{5,1},{9,5},{13,9},{6,2},{10,6},{14,10},{7,3},{... | collective-permute-start | bytes 13832 | tf_op jit(solution)/shard_map/ppermute | solution.py:20
  40.4 19.1 %collective-permute-start.8 = (f32[4,18,16,1]{1,2,3,0:T(8,128)S(1)}, f32[4,18,16,1]{1,2,3,0:T(8,128)S(1)}, u32[]{:S(2)}, u32[]{:S(2)}) collective-permute-start(f32[4,18,16,1]{1,2,3,0:T(8,128)S(1)} %copy.1872), channel_id=1, source_target_pairs={{0,4},{4,8},{8,12},{1,5},{5,9},{9,13},{2,6},{6,10},{10,14},{3,7},{... | collective-permute-start | bytes 13832 | tf_op jit(solution)/shard_map/ppermute | solution.py:17
  97.8 8.1 collective-permute-start.15
  99.1 8.5 collective-permute-start.14
  121.5 8.8 collective-permute-start.21
  122.8 8.7 collective-permute-start.20
  147.8 6.3 collective-permute-start.26
  152.2 6.3 collective-permute-start.27
  165.2 50.5 %collective-permute-start.31 = (f32[4,1,4,32]{0,3,2,1:T(8,128)S(1)}, f32[4,1,4,32]{0,3,2,1:T(8,128)S(1)}, u32[]{:S(2)}, u32[]{:S(2)}) collective-permute-start(f32[4,1,4,32]{0,3,2,1:T(8,128)S(1)} %get-tuple-element.127), channel_id=1, source_target_pairs={{0,16},{1,17},{2,18},{3,19},{4,20},{5,21},{6,22},{7,23},{8,24},{9,... | collective-permute-start | bytes 6152 | tf_op jit(solution)/shard_map/ppermute | solution.py:17
  166.8 49.0 %collective-permute-start.30 = (f32[4,1,4,32]{0,3,2,1:T(8,128)S(1)}, f32[4,1,4,32]{0,3,2,1:T(8,128)S(1)}, u32[]{:S(2)}, u32[]{:S(2)}) collective-permute-start(f32[4,1,4,32]{0,3,2,1:T(8,128)S(1)} %get-tuple-element.128), channel_id=1, source_target_pairs={{16,0},{17,1},{18,2},{19,3},{20,4},{21,5},{22,6},{23,7},{24,8},{25... | collective-permute-start | bytes 6152 | tf_op jit(solution)/shard_map/ppermute | solution.py:20
  296.0 6.7 collective-permute-start.42
  326.9 7.2 collective-permute-start.51
  328.2 7.4 collective-permute-start.50
  350.6 7.4 collective-permute-start.57
  351.9 7.5 collective-permute-start.56
  359.7 6.3 collective-permute-start.58
  395.9 6.5 collective-permute-start.63
  397.7 6.3 collective-permute-start.62
  409.4 7.2 collective-permute-start.64
  425.8 6.6 collective-permute-start.69
  427.6 6.4 collective-permute-start.68
  451.8 6.6 collective-permute-start.75
  453.6 6.4 collective-permute-start.74
  522.6 6.3 collective-permute-start.81
  548.2 6.6 collective-permute-start.87
  550.0 6.4 collective-permute-start.86
  598.5 8.4 collective-permute-start.93
  599.8 8.8 collective-permute-start.92
  622.1 8.8 collective-permute-start.99
  623.4 8.7 collective-permute-start.98
  652.0 6.3 collective-permute-start.104
  656.4 6.3 collective-permute-start.105
  663.8 6.9 collective-permute-start.106
  766.3 7.0 collective-permute-start.118
  767.6 6.4 collective-permute-start.119
  792.7 6.9 collective-permute-start.124
  813.7 7.2 collective-permute-start.129
  815.0 7.4 collective-permute-start.128
  835.6 9.1 collective-permute-start.135
  836.9 8.9 collective-permute-start.134
  881.2 6.8 collective-permute-start.141
  883.0 6.6 collective-permute-start.140
  892.5 7.2 collective-permute-start.142
  908.9 6.8 collective-permute-start.147
  910.7 6.4 collective-permute-start.146
  979.4 6.3 collective-permute-start.153
  (128 other events, 821.3 us)
where the time goes:
time: 1090 us; the launch traced here: 1080 us
  starting transfers between devices  340 us (31%)
  blocking collectives  298 us (27%)
  waiting for transfers between devices  234 us (21%)
  local copies, waits for them, and re-layouts  131 us (12%)
  other arithmetic  74.1 us (7%)
    ppermute x78, starting transfers between devices, extended(): lax.ppermute(lax.slice_in_dim(block, block.shape[dim] - width, None, axis...  238 us
    ppermute x78, waiting for transfers between devices, extended(): lax.ppermute(lax.slice_in_dim(block, 0, width, axis=dim), axis, backward)  195 us
    ppermute x78, starting transfers between devices, extended(): lax.ppermute(lax.slice_in_dim(block, 0, width, axis=dim), axis, backward)  101 us
    all_gather x2, blocking collectives, coarsest(): lax.all_gather(rhs_field[None], ('gx', 'gy', 'gz'), axis=0, tiled=True)  84.7 us
    psum x2, blocking collectives, precond_sum(): return lax.psum(local_dot(first_field, second_field), ('gx', 'gy', 'gz'))  83.3 us
    all_gather x1, blocking collectives, per_device(): lax.all_gather(diagonals[LEVELS][None], ('gx', 'gy', 'gz'), axis=0, tiled...  47.4 us
    psum x1, blocking collectives, per_device(): lax.psum(local_dot(search, operated), ('gx', 'gy', 'gz'))  41.6 us
    psum x1, blocking collectives, per_device(): squares = lax.psum(local_dot(residual, residual), ('gx', 'gy', 'gz'))  41.2 us
  transfers between devices with their start and end apart: 156, of which 111 were waited for; matrix products, arithmetic and copies ran while one was open for 3% of the time, Pallas kernels for 0%

commit v1 on v0

--- a/solution.py
+++ b/solution.py
@@ -7,6 +7,11 @@
 COARSE_SWEEPS = 8
 ITERS = 2
 damping = 0.8
+
+
+def by_each_axis(array, first, second):
+    inner = lax.psum(array, first)
+    return lax.psum(inner, second)
 
 
 def extended(block, sides, width):
@@ -149,7 +154,7 @@
     fine_diag = diagonals[0]
 
     def precond_sum(first_field, second_field):
-        return lax.psum(local_dot(first_field, second_field), ("gx", "gy", "gz"))
+        return by_each_axis(local_dot(first_field, second_field), ("gy", "gz"), "gx")
 
     precond = vcycle(residual, 0)
     precond_dot = precond_sum(residual, precond)

time: 1090 us -> 1120 us (1.028)
  blocking collectives: 298 us -> 326 us
    psum x1 -> x2, blocking collectives: 41.6 us -> 76.8 us  [per_device(): lax.psum(local_dot(search, operated), ('gx', 'gy', 'gz'))]
    psum x2 -> x4, blocking collectives: 83.3 us -> 78.6 us  [the longest x2 68.5 us: by_each_axis(): inner = lax.psum(array, first)]
where the time goes in v1:
time: 1120 us; the launch traced here: 1100 us
  starting transfers between devices  338 us (30%)
  blocking collectives  326 us (29%)
  waiting for transfers between devices  230 us (21%)
  local copies, waits for them, and re-layouts  131 us (12%)
  other arithmetic  74 us (7%)
    ppermute x78, starting transfers between devices, extended(): lax.ppermute(lax.slice_in_dim(block, block.shape[dim] - width, None, axis...  237 us
    ppermute x78, waiting for transfers between devices, extended(): lax.ppermute(lax.slice_in_dim(block, 0, width, axis=dim), axis, backward)  191 us
    ppermute x78, starting transfers between devices, extended(): lax.ppermute(lax.slice_in_dim(block, 0, width, axis=dim), axis, backward)  101 us
    all_gather x2, blocking collectives, coarsest(): lax.all_gather(rhs_field[None], ('gx', 'gy', 'gz'), axis=0, tiled=True)  84.7 us
    psum x2, blocking collectives, per_device(): lax.psum(local_dot(search, operated), ('gx', 'gy', 'gz'))  76.8 us
    psum x2, blocking collectives, by_each_axis(): inner = lax.psum(array, first)  68.5 us
    all_gather x1, blocking collectives, per_device(): lax.all_gather(diagonals[LEVELS][None], ('gx', 'gy', 'gz'), axis=0, tiled...  47.4 us
    ppermute x78, waiting for transfers between devices, extended(): lax.ppermute(lax.slice_in_dim(block, block.shape[dim] - width, None, axis...  39.3 us
  transfers between devices with their start and end apart: 156, of which 111 were waited for; matrix products, arithmetic and copies ran while one was open for 3% of the time, Pallas kernels for 0%

profile of v1, /device:TPU:0, one launch (start us, length us, event | category | flops | bytes accessed | tf_op | source)
XLA Modules:
  0.0 1102.3 jit_solution(16106617621000621389)
XLA Ops:
  2.7 4.9 collective-permute-start.1
  16.0 4.5 collective-permute-start.2
  40.4 4.8 collective-permute-start.8
  45.2 9.7 reshape.124
  69.1 8.8 copy.1882
  77.9 11.7 %reduce_sum.126 = f32[4,8,8,64]{0,3,2,1:T(8,128)S(1)} reduce(f32[4,8,2,8,2,64,2]{0,6,5,4,3,2,1:T(2,128)} %bitcast.21, f32[]{:T(128)} %constant.28.clone.1), dimensions={2,4,6}, to_apply=%region_0.0 | reduce | flops 114688 | bytes 589828 | tf_op jit(solution)/shard_map/reduce_sum | solution.py:43
  99.1 4.6 collective-permute-start.14
  117.1 4.3 collective-permute-done.18
  122.8 4.7 collective-permute-start.20
  147.8 4.4 collective-permute-start.26
  154.1 4.4 collective-permute-done.27
  168.1 47.4 %all-gather.1 = f32[64,2,16]{2,1,0:T(2,128)S(1)} all-gather(f32[2,2,16]{2,1,0:T(2,128)S(1)} %multiply_add_fusion.3), channel_id=3, replica_groups=mesh['gx'=2,'gy'=4,'gz'=4] {'gx','gy','gz'}, dimensions={0}, use_global_device_ids=true | all-gather | bytes 8448 | tf_op jit(solution)/shard_map/all_gather | solution.py:111
  230.6 40.6 %all-gather = f32[128,2,2,16]{3,2,1,0:T(2,128)S(1)} all-gather(f32[4,2,2,16]{3,2,1,0:T(2,128)S(1)} %copy.1905), channel_id=2, replica_groups=mesh['gx'=2,'gy'=4,'gz'=4] {'gx','gy','gz'}, dimensions={0}, use_global_device_ids=true | all-gather | bytes 33792 | tf_op jit(solution)/shard_map/all_gather | solution.py:118
  328.2 4.6 collective-permute-start.50
  337.1 4.6 collective-permute-start.53
  351.9 4.7 collective-permute-start.56
  361.0 5.0 collective-permute-start.59
  369.5 7.8 broadcast_in_dim.14
  377.3 10.0 copy.1931
  397.7 4.7 collective-permute-start.62
  405.1 4.3 collective-permute-start.65
  410.8 5.8 collective-permute-done.64
  427.6 4.8 collective-permute-start.68
  453.6 4.8 collective-permute-start.74
  469.7 34.3 %psum.49 = f32[4]{0:T(128)S(1)} all-reduce(f32[4]{0:T(128)S(1)} %get-tuple-element.13), channel_id=1, replica_groups=mesh['gx'=2,'gy'=4,'gz'=4] {'gy','gz'}, use_global_device_ids=true, to_apply=%region_7.8 | all-reduce | flops 4 | bytes 32 | tf_op jit(solution)/shard_map/psum | solution.py:13
  504.0 36.8 %psum.51 = f32[4]{0:T(128)S(1)} all-reduce(f32[4]{0:T(128)S(1)} %get-tuple-element.12), channel_id=1, replica_groups=mesh['gx'=2,'gy'=4,'gz'=4] {'gx','gy','gz'}, use_global_device_ids=true, to_apply=%region_10.11 | all-reduce | flops 4 | bytes 32 | tf_op jit(solution)/shard_map/psum | solution.py:164
  540.8 5.1 psum.50
  558.7 5.4 collective-permute-start.80
  583.4 4.8 collective-permute-start.86
  600.2 8.8 copy.1982
  609.0 13.1 %reduce_sum.134 = f32[4,8,8,64]{0,3,2,1:T(8,128)} reduce(f32[4,8,2,8,2,64,2]{0,6,5,4,3,2,1:T(2,128)} %bitcast.23, f32[]{:T(128)} %constant.28.clone.1), dimensions={2,4,6}, to_apply=%region_11.12 | reduce | flops 114688 | bytes 589828 | tf_op jit(solution)/shard_map/reduce_sum | solution.py:43
  633.1 4.9 collective-permute-start.92
  656.7 4.7 collective-permute-start.98
  685.3 4.4 collective-permute-start.104
  691.6 4.4 collective-permute-done.105
  735.1 44.2 %all-gather.2 = f32[128,2,2,16]{3,2,1,0:T(2,128)S(1)} all-gather(f32[4,2,2,16]{3,2,1,0:T(2,128)S(1)} %copy.2005), channel_id=4, replica_groups=mesh['gx'=2,'gy'=4,'gz'=4] {'gx','gy','gz'}, dimensions={0}, use_global_device_ids=true | all-gather | bytes 33792 | tf_op jit(solution)/shard_map/all_gather | solution.py:118
  848.2 4.6 collective-permute-start.128
  870.1 5.0 collective-permute-start.134
  886.9 8.9 broadcast_in_dim.17
  895.8 10.0 copy.2029
  916.2 5.0 collective-permute-start.140
  927.1 5.8 collective-permute-done.142
  944.0 5.1 collective-permute-start.146
  960.1 34.3 %psum.52 = f32[4]{0:T(128)S(1)} all-reduce(f32[4]{0:T(128)S(1)} %get-tuple-element.16), channel_id=1, replica_groups=mesh['gx'=2,'gy'=4,'gz'=4] {'gy','gz'}, use_global_device_ids=true, to_apply=%region_15.16 | all-reduce | flops 4 | bytes 32 | tf_op jit(solution)/shard_map/psum | solution.py:13
  994.4 4.9 psum.53
  1009.7 4.5 collective-permute-start.152
  1022.4 40.0 %psum.54 = f32[4]{0:T(128)S(1)} all-reduce(f32[4]{0:T(128)S(1)} %get-tuple-element.14), channel_id=1, replica_groups=mesh['gx'=2,'gy'=4,'gz'=4] {'gx','gy','gz'}, use_global_device_ids=true, to_apply=%region_18.19 | all-reduce | flops 4 | bytes 32 | tf_op jit(solution)/shard_map/psum | solution.py:164
  1063.4 38.1 %psum.55 = f32[4]{0:T(128)S(1)} all-reduce(f32[4]{0:T(128)S(1)} %get-tuple-element.197), channel_id=1, replica_groups=mesh['gx'=2,'gy'=4,'gz'=4] {'gx','gy','gz'}, use_global_device_ids=true, to_apply=%region_20.21 | all-reduce | flops 4 | bytes 32 | tf_op jit(solution)/shard_map/psum | solution.py:172
  (674 shorter events, 545.2 us)
Async XLA Ops:
  2.7 6.5 collective-permute-start.1
  14.2 6.3 collective-permute-start.3
  38.6 20.4 %collective-permute-start.9 = (f32[4,18,16,1]{1,2,3,0:T(8,128)S(1)}, f32[4,18,16,1]{1,2,3,0:T(8,128)S(1)}, u32[]{:S(2)}, u32[]{:S(2)}) collective-permute-start(f32[4,18,16,1]{1,2,3,0:T(8,128)S(1)} %copy.1873), channel_id=1, source_target_pairs={{4,0},{8,4},{12,8},{5,1},{9,5},{13,9},{6,2},{10,6},{14,10},{7,3},{... | collective-permute-start | bytes 13832 | tf_op jit(solution)/shard_map/ppermute | solution.py:25
  40.4 19.1 %collective-permute-start.8 = (f32[4,18,16,1]{1,2,3,0:T(8,128)S(1)}, f32[4,18,16,1]{1,2,3,0:T(8,128)S(1)}, u32[]{:S(2)}, u32[]{:S(2)}) collective-permute-start(f32[4,18,16,1]{1,2,3,0:T(8,128)S(1)} %copy.1872), channel_id=1, source_target_pairs={{0,4},{4,8},{8,12},{1,5},{5,9},{9,13},{2,6},{6,10},{10,14},{3,7},{... | collective-permute-start | bytes 13832 | tf_op jit(solution)/shard_map/ppermute | solution.py:22
  97.8 8.1 collective-permute-start.15
  99.1 8.5 collective-permute-start.14
  121.5 8.8 collective-permute-start.21
  122.8 8.7 collective-permute-start.20
  147.8 6.3 collective-permute-start.26
  152.2 6.3 collective-permute-start.27
  165.1 50.5 %collective-permute-start.31 = (f32[4,1,4,32]{0,3,2,1:T(8,128)S(1)}, f32[4,1,4,32]{0,3,2,1:T(8,128)S(1)}, u32[]{:S(2)}, u32[]{:S(2)}) collective-permute-start(f32[4,1,4,32]{0,3,2,1:T(8,128)S(1)} %get-tuple-element.125), channel_id=1, source_target_pairs={{0,16},{1,17},{2,18},{3,19},{4,20},{5,21},{6,22},{7,23},{8,24},{9,... | collective-permute-start | bytes 6152 | tf_op jit(solution)/shard_map/ppermute | solution.py:22
  166.8 49.0 %collective-permute-start.30 = (f32[4,1,4,32]{0,3,2,1:T(8,128)S(1)}, f32[4,1,4,32]{0,3,2,1:T(8,128)S(1)}, u32[]{:S(2)}, u32[]{:S(2)}) collective-permute-start(f32[4,1,4,32]{0,3,2,1:T(8,128)S(1)} %get-tuple-element.126), channel_id=1, source_target_pairs={{16,0},{17,1},{18,2},{19,3},{20,4},{21,5},{22,6},{23,7},{24,8},{25... | collective-permute-start | bytes 6152 | tf_op jit(solution)/shard_map/ppermute | solution.py:25
  296.0 6.7 collective-permute-start.42
  326.9 7.2 collective-permute-start.51
  328.2 7.4 collective-permute-start.50
  350.6 7.4 collective-permute-start.57
  351.9 7.5 collective-permute-start.56
  359.7 6.3 collective-permute-start.58
  395.9 6.5 collective-permute-start.63
  409.4 7.2 collective-permute-start.64
  425.8 6.6 collective-permute-start.69
  427.6 6.4 collective-permute-start.68
  451.8 6.6 collective-permute-start.75
  453.6 6.4 collective-permute-start.74
  557.0 7.2 collective-permute-start.81
  558.7 7.0 collective-permute-start.80
  581.6 6.6 collective-permute-start.87
  583.4 6.4 collective-permute-start.86
  631.8 8.4 collective-permute-start.93
  633.1 8.8 collective-permute-start.92
  655.4 8.8 collective-permute-start.99
  656.7 8.7 collective-permute-start.98
  685.3 6.3 collective-permute-start.104
  689.7 6.3 collective-permute-start.105
  697.1 6.9 collective-permute-start.106
  799.6 7.0 collective-permute-start.118
  800.9 6.4 collective-permute-start.119
  825.9 6.9 collective-permute-start.124
  846.9 7.2 collective-permute-start.129
  848.2 7.4 collective-permute-start.128
  868.8 9.1 collective-permute-start.135
  870.1 9.0 collective-permute-start.134
  914.4 6.8 collective-permute-start.141
  916.2 6.6 collective-permute-start.140
  925.7 7.2 collective-permute-start.142
  942.2 6.8 collective-permute-start.147
  944.0 6.4 collective-permute-start.146
  1007.9 6.3 collective-permute-start.153
  (128 other events, 814.1 us)
